TPU v7x, 32 devices: a whole 2x2x4 slice. The times are simulated.
32 devices in a mesh: ea: 4 (over y, x), row: 4 (over z), col: 2 (over core).
Axes of the slice: x: 2, y: 2, z: 4, core: 2. Of those that a mesh axis runs over, the one named last changes fastest.
Arguments:
- weights: float32 [4, 256, 2048], P('ea', 'row', 'col'), parts along dimension 0, may hold values from -6 to 6
- codebook: float32 [4, 16, 2, 256], P('ea', 'col'), parts along dimension 0, may hold values from -4 to 4
- assign: int32 [4, 256, 1024], P('ea', 'row', 'col'), parts along dimension 0, may hold values from 0 to 255
- chol_upper: float32 [4, 2048, 2048], P('ea', 'row', 'col'), parts along dimension 0, may hold values from 0 to 1.4, as said below
- inv_blocks: float32 [4, 16, 128, 128], P('ea', 'col'), parts along dimension 0, may hold values from -1 to 1.5, as said below
Outputs:
- errors: float32 [4, 256, 2048], P('ea', 'row', 'col'), parts along dimension 0
- row_loss: float32 [4, 256], P('ea', 'row'), parts along dimension 0
- codeword_mass: float32 [4, 16, 256], P('ea', 'col'), parts along dimension 0
There are 4 independent parts, one for each index of `ea`. A program takes and returns all parts, laid end to end along the dimension named above; each array names one. Nothing has to cross between parts.
Inputs may be any that keep to these rules, and one draw needn't show every extreme that they name: `chol_upper`: upper triangular with a positive diagonal. inv_blocks[x, b] is the inverse of the diagonal block of chol_upper[x] on rows and columns [b * 128, (b + 1) * 128).
All inputs are finite; a program needn't handle non-finite values.
Results may differ from a plain program's by a relative error of at most 0.0001.
Values sent between devices are 32-bit elements; how exact they have to be, the bound alone decides.
A program may use at most 64 MiB of HBM per device.

v0:
```python
import jax
import jax.numpy as jnp
from jax import lax
from jax.sharding import PartitionSpec as P


def from_root(value, axis, source):
    kept = jnp.where(lax.axis_index(axis) == source, value, 0).astype(value.dtype)
    return lax.psum(kept, axis)


def flat_labels(assign, half_block, code_count):
    pair_count = assign.shape[2]
    offsets = jnp.arange(pair_count, dtype=jnp.int32) // half_block * code_count
    return assign + offsets[None, None, :]


def lookup_local(codebook, labels):
    experts, row_count, pair_count = labels.shape
    code_table = jnp.transpose(codebook, (0, 2, 1, 3)).reshape(experts, 2, -1)

    def select(rows_table, indices):
        return jnp.stack(
            [jnp.take(rows_table[0], indices), jnp.take(rows_table[1], indices)], axis=-1
        )

    picked = jax.vmap(select)(code_table, labels)
    return picked.reshape(experts, row_count, 2 * pair_count)


def mass_by_code(errors, labels, local_blocks, code_count):
    experts, row_count, width = errors.shape
    squared = errors * errors
    paired = squared.reshape(experts, row_count, width // 2, 2).sum(axis=3)

    def summed(values, marks):
        return jax.ops.segment_sum(
            values.reshape(-1), marks.reshape(-1), num_segments=local_blocks * code_count
        )

    return jax.vmap(summed)(paired, labels).reshape(experts, local_blocks, code_count)


def local(weights, codebook, assign, chol_upper, inv_blocks):
    block_size = inv_blocks.shape[2]
    local_blocks = inv_blocks.shape[1]
    local_width = weights.shape[2]
    code_count = codebook.shape[3]
    column_rank = lax.axis_index("col")
    block_total = local_blocks * lax.axis_size("col")
    labels = flat_labels(assign, block_size // 2, code_count)
    quantized = lookup_local(codebook, labels)
    column_ids = column_rank * local_width + jnp.arange(local_width, dtype=jnp.int32)
    stacked = lax.all_gather(chol_upper, "row", axis=1, tiled=True)

    def panel_of(number):
        return lax.dynamic_slice_in_dim(stacked, number * block_size, block_size, 1)

    def own_block(current, number):
        return lax.dynamic_slice_in_dim(current, number % local_blocks * block_size, block_size, 2)

    def block_error(current_block, number):
        owner_rank = number // local_blocks
        inverse = lax.dynamic_index_in_dim(inv_blocks, number % local_blocks, 1, keepdims=False)
        target = own_block(quantized, number)

        def compute():
            return jnp.einsum(
                "xrc,xcd->xrd", current_block - target, inverse, precision=lax.Precision.HIGHEST
            )

        def nothing():
            return jnp.zeros(current_block.shape, jnp.float32)

        computed = lax.cond(owner_rank == column_rank, compute, nothing)
        return from_root(computed, "col", owner_rank)

    def propagate(current, error_block, panel_rows, number, targets):
        beyond = targets >= (number + 1) * block_size
        masked = jnp.where(beyond[None, None, :], panel_rows, 0.0)
        return current - jnp.einsum(
            "xrc,xcd->xrd", error_block, masked, precision=lax.Precision.HIGHEST
        )

    def record(errors, error_block, number):
        owner_rank = number // local_blocks
        offset = number % local_blocks * block_size
        previous = lax.dynamic_slice_in_dim(errors, offset, block_size, 2)
        chosen = jnp.where(owner_rank == column_rank, error_block, previous)
        return lax.dynamic_update_slice_in_dim(errors, chosen, offset, 2)

    blank = jnp.zeros(weights.shape, jnp.float32)

    def advance(number, state_pair):
        current, errors = state_pair
        error_block = block_error(own_block(current, number), number)
        errors = record(errors, error_block, number)
        current = propagate(current, error_block, panel_of(number), number, column_ids)
        return (current, errors)

    current, errors = lax.fori_loop(0, block_total, advance, (weights, blank))
    row_loss = lax.psum(jnp.sum(errors * errors, axis=2), "col")
    local_mass = mass_by_code(errors, labels, local_blocks, code_count)
    codeword_mass = lax.psum(local_mass, "row")
    return (errors, row_loss, codeword_mass)


def solution(mesh):
    return jax.shard_map(
        local,
        mesh=mesh,
        in_specs=(
            P("ea", "row", "col"),
            P("ea", "col", None, None),
            P("ea", "row", "col"),
            P("ea", "row", "col"),
            P("ea", "col", None, None),
        ),
        out_specs=(P("ea", "row", "col"), P("ea", "row"), P("ea", "col", None)),
        check_vma=False,
    )
```

profile of v0, /device:TPU:0, one launch (start us, length us, event | category | flops | bytes accessed | tf_op | source)
XLA Modules:
  0.0 742.4 jit_solution(10534728693327028452)
XLA Ops:
  9.9 190.2 %gather_fusion.1 = f32[32768]{0:T(1024)S(1)} fusion(f32[1,2048]{1,0:T(1,128)S(1)} %get-tuple-element.332, s32[32768]{0:T(1024)S(1)} %bitcast.50), kind=kCustom, calls=%fused_computation.1.clone | custom fusion | bytes 524288 | tf_op jit(solution)/shard_map/vmap(jit(_take))/gather | solution.py:24
  200.2 190.2 %gather_fusion = f32[32768]{0:T(1024)S(1)} fusion(f32[1,2048]{1,0:T(1,128)S(1)} %get-tuple-element.333, s32[32768]{0:T(1024)S(1)} %bitcast.51), kind=kCustom, calls=%fused_computation.clone | custom fusion | bytes 524288 | tf_op jit(solution)/shard_map/vmap(jit(_take))/gather | solution.py:24
  392.2 98.7 %while.18 = (s32[]{:T(128)}, f32[1,64,1024]{2,1,0:T(8,128)S(1)}, f32[1,64,1024]{2,1,0:T(8,128)S(1)}, s32[]{:T(128)}, f32[1,64,1024]{2,1,0:T(8,128)S(1)}, /*index...) while((s32[]{:T(128)}, f32[1,64,1024]{2,1,0:T(8,128)S(1)}, ...), condition=%wide.region_4.6_spmd.clone, body=%wide.region_0.5_spmd.clone.sunk | while | flops 113477664 | bytes 1477659 | solution.py:101
  393.4 3.4 psum.32
  396.8 1.5 fusion.35
  399.6 3.4 psum.32
  403.0 1.5 fusion.35
  405.7 3.4 psum.32
  411.9 3.4 psum.32
  418.0 3.4 psum.32
  424.2 3.4 psum.32
  427.6 1.5 fusion.35
  430.3 3.4 psum.32
  433.8 1.5 fusion.35
  436.5 3.4 psum.32
  439.9 1.5 fusion.35
  441.6 4.6 psum.32
  447.9 4.5 psum.32
  452.4 1.5 fusion.35
  454.1 4.5 psum.32
  458.5 1.5 fusion.35
  460.2 4.5 psum.32
  464.7 1.5 fusion.35
  466.4 4.5 psum.32
  472.5 4.5 psum.32
  477.0 1.5 fusion.35
  478.7 4.5 psum.32
  483.2 1.5 fusion.35
  484.8 4.5 psum.32
  491.0 3.0 psum.28
  495.0 226.3 %scatter_custom_fusion = f32[2048]{0:T(1024)S(1)} fusion(s32[32768]{0:T(1024)S(1)} %broadcast_select_fusion.1, f32[32768]{0:T(1024)S(1)} %bitcast.55, f32[]{:T(128)} %constant.181.clone.1), kind=kCustom, calls=%fused_computation.45 | custom fusion | flops 32768 | bytes 8196
  721.4 14.2 %psum.29 = f32[1,8,256]{2,1,0:T(8,128)} all-reduce(f32[1,8,256]{2,1,0:T(8,128)S(1)} %reshape.106), channel_id=1, replica_groups=mesh['ea'=4,'row'=4,'col'=2] {'row'}, use_global_device_ids=true, to_apply=%region_9.11 | all-reduce | flops 2048 | bytes 16384 | tf_op jit(solution)/shard_map/psum | solution.py:104
  (121 shorter events, 32.9 us)
Async XLA Ops:
  7.2 385.0 %all-gather.2.cloned.1.call-start = ((), (), s32[]{:S(2)}) async-start(), calls=%async_computation | async-start | bytes 10485760 | tf_op jit(solution)/shard_map/all_gather | solution.py:54
  200.2 190.9 %copy-start.3 = (s32[2]{0:T(128)S(1)}, s32[2]{0:T(128)}, u32[]{:S(2)}) copy-start(s32[2]{0:T(128)} %constant.194) | copy-start | bytes 28
  200.2 191.3 %copy-start.2 = (s32[2]{0:T(128)S(1)}, s32[2]{0:T(128)}, u32[]{:S(2)}) copy-start(s32[2]{0:T(128)} %constant.197) | copy-start | bytes 28
  200.2 192.0 %copy-start = (f32[1,64,1024]{2,1,0:T(8,128)S(1)}, f32[1,64,1024]{2,1,0:T(8,128)}, u32[]{:S(2)}) copy-start(f32[1,64,1024]{2,1,0:T(8,128)} %param.11) | copy-start | bytes 786436
  490.9 244.6 %copy-start.1 = (f32[1,64,1024]{2,1,0:T(8,128)}, f32[1,64,1024]{2,1,0:T(8,128)S(1)}, u32[]{:S(2)}) copy-start(f32[1,64,1024]{2,1,0:T(8,128)S(1)} %get-tuple-element.263) | copy-start | bytes 786436
Sparse Core Ops, SparseCore 0:
  9.5 152.3 all-gather.1
where the time goes:
time: 744 us; the launch traced here: 742 us
  local copies, waits for them, and re-layouts  382 us (51%)
  other arithmetic  230 us (31%)
  blocking collectives  80.4 us (11%)
  matrix products  33.1 us (4%)
  between operations  14.3 us (2%)
    unnamed x5, other arithmetic  227 us
    gather x3, local copies, waits for them, and re-layouts, select(): jnp.take(rows_table[0], indices)  190 us
    gather x2, local copies, waits for them, and re-layouts, select(): jnp.take(rows_table[1], indices)  190 us
    psum x16, blocking collectives, from_root(): return lax.psum(kept, axis)  63.3 us
    dot_general x16, matrix products, propagate(): jnp.einsum('xrc,xcd->xrd', error_block, masked, precision=lax.Precision.H...  24.4 us
  transfers between devices with their start and end apart: 1, of which 0 were waited for; matrix products, arithmetic and copies ran while one was open for 52% of the time, Pallas kernels for 0%

commit v1 on v0

--- a/solution.py
+++ b/solution.py
@@ -6,7 +6,7 @@
 
 def from_root(value, axis, source):
     kept = jnp.where(lax.axis_index(axis) == source, value, 0).astype(value.dtype)
-    return lax.psum(kept, axis)
+    return jnp.sum(lax.all_gather(kept, axis), axis=0)
 
 
 def flat_labels(assign, half_block, code_count):

time: 744 us -> 719 us (0.966)
  blocking collectives: 80.4 us -> 55.3 us
    psum x16 -> x0, blocking collectives: 63.3 us -> none  [from_root(): return lax.psum(kept, axis)]
    all_gather x0 -> x16, blocking collectives: none -> 38.1 us  [from_root(): return jnp.sum(lax.all_gather(kept, axis), axis=0)]
  transfers between devices with their start and end apart: 1 -> 1, of which waited for: 0 -> 0; matrix products, arithmetic and copies ran while one was open for 52% -> 54% of each run, Pallas kernels for 0% -> 0%
where the time goes in v1:
time: 719 us; the launch traced here: 717 us
  local copies, waits for them, and re-layouts  382 us (53%)
  other arithmetic  230 us (32%)
  blocking collectives  55.3 us (8%)
  matrix products  33 us (5%)
  between operations  14.3 us (2%)
    unnamed x5, other arithmetic  227 us
    gather x3, local copies, waits for them, and re-layouts, select(): jnp.take(rows_table[0], indices)  190 us
    gather x2, local copies, waits for them, and re-layouts, select(): jnp.take(rows_table[1], indices)  190 us
    all_gather x16, blocking collectives, from_root(): return jnp.sum(lax.all_gather(kept, axis), axis=0)  38.1 us
    dot_general x16, matrix products, propagate(): jnp.einsum('xrc,xcd->xrd', error_block, masked, precision=lax.Precision.H...  24.3 us
  transfers between devices with their start and end apart: 1, of which 0 were waited for; matrix products, arithmetic and copies ran while one was open for 54% of the time, Pallas kernels for 0%

profile of v1, /device:TPU:0, one launch (start us, length us, event | category | flops | bytes accessed | tf_op | source)
XLA Modules:
  0.0 717.2 jit_solution(10817993993569206558)
XLA Ops:
  9.9 190.2 %gather_fusion.1 = f32[32768]{0:T(1024)S(1)} fusion(f32[1,2048]{1,0:T(1,128)S(1)} %get-tuple-element.332, s32[32768]{0:T(1024)S(1)} %bitcast.54), kind=kCustom, calls=%fused_computation.1.clone | custom fusion | bytes 524288 | tf_op jit(solution)/shard_map/vmap(jit(_take))/gather | solution.py:24
  200.2 190.2 %gather_fusion = f32[32768]{0:T(1024)S(1)} fusion(f32[1,2048]{1,0:T(1,128)S(1)} %get-tuple-element.333, s32[32768]{0:T(1024)S(1)} %bitcast.55), kind=kCustom, calls=%fused_computation.clone | custom fusion | bytes 524288 | tf_op jit(solution)/shard_map/vmap(jit(_take))/gather | solution.py:24
  392.2 73.4 %while.18 = (s32[]{:T(128)}, f32[1,64,1024]{2,1,0:T(8,128)S(1)}, f32[1,64,1024]{2,1,0:T(8,128)S(1)}, s32[]{:T(128)}, f32[1,64,1024]{2,1,0:T(8,128)S(1)}, /*index...) while((s32[]{:T(128)}, f32[1,64,1024]{2,1,0:T(8,128)S(1)}, ...), condition=%wide.region_4.6_spmd.clone, body=%wide.region_0.5_spmd.clone.sunk | while | flops 113477664 | bytes 1608743 | solution.py:101
  393.4 1.9 all-gather.3
  395.3 1.5 fusion.37
  398.0 1.9 all-gather.3
  399.9 1.5 fusion.37
  402.6 1.9 all-gather.3
  404.5 1.5 fusion.37
  407.2 1.9 all-gather.3
  409.1 1.5 fusion.37
  411.8 1.9 all-gather.3
  413.7 1.5 fusion.37
  416.4 1.9 all-gather.3
  418.3 1.5 fusion.37
  421.0 1.9 all-gather.3
  422.9 1.5 fusion.37
  425.6 1.9 all-gather.3
  427.5 1.5 fusion.37
  429.1 2.7 all-gather.3
  431.9 1.5 fusion.37
  433.5 2.9 all-gather.3
  438.1 2.9 all-gather.3
  441.1 1.5 fusion.37
  442.7 2.9 all-gather.3
  447.3 2.9 all-gather.3
  451.9 2.9 all-gather.3
  456.6 2.9 all-gather.3
  461.2 2.9 all-gather.3
  465.8 3.0 psum.14
  469.8 226.3 %scatter_custom_fusion = f32[2048]{0:T(1024)S(1)} fusion(s32[32768]{0:T(1024)S(1)} %broadcast_select_fusion.1, f32[32768]{0:T(1024)S(1)} %bitcast.59, f32[]{:T(128)} %constant.181.clone.1), kind=kCustom, calls=%fused_computation.45 | custom fusion | flops 32768 | bytes 8196
  696.1 14.2 %psum.15 = f32[1,8,256]{2,1,0:T(8,128)} all-reduce(f32[1,8,256]{2,1,0:T(8,128)S(1)} %reshape.106), channel_id=1, replica_groups=mesh['ea'=4,'row'=4,'col'=2] {'row'}, use_global_device_ids=true, to_apply=%region_9.11 | all-reduce | flops 2048 | bytes 16384 | tf_op jit(solution)/shard_map/psum | solution.py:104
  (137 shorter events, 32.9 us)
Async XLA Ops:
  7.2 385.0 %all-gather.6.cloned.1.call-start = ((), (), s32[]{:S(2)}) async-start(), calls=%async_computation | async-start | bytes 10485760 | tf_op jit(solution)/shard_map/all_gather | solution.py:54
  200.2 190.9 %copy-start.3 = (s32[2]{0:T(128)S(1)}, s32[2]{0:T(128)}, u32[]{:S(2)}) copy-start(s32[2]{0:T(128)} %constant.194) | copy-start | bytes 28
  200.2 191.3 %copy-start.2 = (s32[2]{0:T(128)S(1)}, s32[2]{0:T(128)}, u32[]{:S(2)}) copy-start(s32[2]{0:T(128)} %constant.197) | copy-start | bytes 28
  200.2 192.0 %copy-start = (f32[1,64,1024]{2,1,0:T(8,128)S(1)}, f32[1,64,1024]{2,1,0:T(8,128)}, u32[]{:S(2)}) copy-start(f32[1,64,1024]{2,1,0:T(8,128)} %param.11) | copy-start | bytes 786436
  465.7 244.7 %copy-start.1 = (f32[1,64,1024]{2,1,0:T(8,128)}, f32[1,64,1024]{2,1,0:T(8,128)S(1)}, u32[]{:S(2)}) copy-start(f32[1,64,1024]{2,1,0:T(8,128)S(1)} %get-tuple-element.263) | copy-start | bytes 786436
Sparse Core Ops, SparseCore 0:
  9.5 152.3 all-gather.5
